TPU v7x, 32 devices: a whole 2x2x4 slice. The times are simulated.
32 devices in a mesh: gx: 32 (over z, y, x, core).
Axes of the slice: x: 2, y: 2, z: 4, core: 2. Of those that a mesh axis runs over, the one named last changes fastest.
Arguments:
- value: float32 [64, 48, 32, 128], P('gx'), may hold values from -6 to 6
- target: float32 [64, 48, 32, 128], P('gx'), may hold values from -6 to 6
- obstacle: float32 [64, 48, 32, 128], P('gx'), may hold values from -6 to -0.5
- fractions: float32 [16, 4], replicated, may hold values from 0 to 1
- control_cost: float32 [16], replicated, may hold values from 0 to 0.5
- shard_offset: int32 [16], replicated, may hold values from -8 to 8, as said below
- cell_offset: int32 [16], replicated, may hold values from 0 to 1
- grid_offset: int32 [16, 3], replicated, may hold values from -4 to 4
Outputs:
- updated: float32 [64, 48, 32, 128], P('gx')
Inputs may be any that keep to these rules, and one draw needn't show every extreme that they name: `shard_offset`: every draw holds both -8 and 8.
All inputs are finite; a program needn't handle non-finite values.
Results may differ from a plain program's by a relative error of at most 0.00002.
Values sent between devices are 32-bit elements; how exact they have to be, the bound alone decides.
A program may use at most 128 MiB of HBM per device.

v0:
```python
import jax
import jax.numpy as jnp
from jax import lax
from jax.sharding import PartitionSpec as P

NCTRL = 16
REACH = 8


def passed_along(x, axis, by):
    size = lax.axis_size(axis)
    return lax.ppermute(x, axis, [(i, (i + by) % size) for i in range(size)])


def blend(low, high, frac):
    return (1.0 - frac) * low + frac * high


def body(value, target, obstacle, fractions, control_cost, shard_offset, cell_offset, grid_offset):
    rows = value.shape[0]
    count = 2 * REACH + 2
    above = []
    current = value
    for step in range(REACH + 1):
        current = passed_along(current, "gx", -1)
        above.append(current)
    below = []
    current = value
    for step in range(REACH):
        current = passed_along(current, "gx", 1)
        below.append(current)
    pieces = below[::-1] + [value] + above

    def make_branch(offset):

        def branch(start):
            joined = jnp.concatenate([pieces[offset], pieces[offset + 1]], axis=0)
            return lax.dynamic_slice_in_dim(joined, start, rows + 1, 0)

        return branch

    branches = [make_branch(offset) for offset in range(count - 1)]

    def one_control(u, best):
        needed = lax.switch(shard_offset[u] + REACH, branches, cell_offset[u])
        field = blend(needed[:rows], needed[1:], fractions[u, 0])
        for axis_k in range(1, 4):
            moved = grid_offset[u, axis_k - 1]
            field = blend(
                jnp.roll(field, -moved, axis=axis_k),
                jnp.roll(field, -moved - 1, axis=axis_k),
                fractions[u, axis_k],
            )
        return jnp.minimum(best, field + control_cost[u])

    start = jnp.full(value.shape, jnp.inf, jnp.float32)
    best = lax.fori_loop(0, NCTRL, one_control, start)
    return jnp.maximum(obstacle, jnp.minimum(target, best))


def solution(mesh):
    return jax.shard_map(
        body,
        mesh=mesh,
        in_specs=(
            P("gx", None, None, None),
            P("gx", None, None, None),
            P("gx", None, None, None),
            P(),
            P(),
            P(),
            P(),
            P(),
        ),
        out_specs=P("gx", None, None, None),
        check_vma=False,
    )
```

profile of v0, /device:TPU:3, one launch (start us, length us, event | category | flops | bytes accessed | tf_op | source)
XLA Modules:
  0.0 734.0 jit_solution(4205601633713792120)
XLA Ops:
  2.6 35.1 %collective-permute-done.8 = f32[2,48,32,128]{3,2,1,0:T(8,128)S(1)} collective-permute-done((f32[2,48,32,128]{3,2,1,0:T(8,128)}, f32[2,48,32,128]{3,2,1,0:T(8,128)S(1)}, u32[]{:S(2)}, u32[]{:S(2)}) %collective-permute-start.8) | collective-permute-done | bytes 1572896 | tf_op jit(solution)/shard_map/ppermute | solution.py:12
  41.6 34.4 %collective-permute-done.9 = f32[2,48,32,128]{3,2,1,0:T(8,128)S(1)} collective-permute-done((f32[2,48,32,128]{3,2,1,0:T(8,128)S(1)}, f32[2,48,32,128]{3,2,1,0:T(8,128)S(1)}, u32[]{:S(2)}, u32[]{:S(2)}) %collective-permute-start.9) | collective-permute-done | bytes 1572896 | tf_op jit(solution)/shard_map/ppermute | solution.py:12
  78.6 34.0 %collective-permute-done.10 = f32[2,48,32,128]{3,2,1,0:T(8,128)S(1)} collective-permute-done((f32[2,48,32,128]{3,2,1,0:T(8,128)S(1)}, f32[2,48,32,128]{3,2,1,0:T(8,128)S(1)}, u32[]{:S(2)}, u32[]{:S(2)}) %collective-permute-start.10) | collective-permute-done | bytes 1572896 | tf_op jit(solution)/shard_map/ppermute | solution.py:12
  115.4 33.1 %collective-permute-done.11 = f32[2,48,32,128]{3,2,1,0:T(8,128)S(1)} collective-permute-done((f32[2,48,32,128]{3,2,1,0:T(8,128)S(1)}, f32[2,48,32,128]{3,2,1,0:T(8,128)S(1)}, u32[]{:S(2)}, u32[]{:S(2)}) %collective-permute-start.11) | collective-permute-done | bytes 1572896 | tf_op jit(solution)/shard_map/ppermute | solution.py:12
  151.2 32.2 %collective-permute-done.12 = f32[2,48,32,128]{3,2,1,0:T(8,128)S(1)} collective-permute-done((f32[2,48,32,128]{3,2,1,0:T(8,128)S(1)}, f32[2,48,32,128]{3,2,1,0:T(8,128)S(1)}, u32[]{:S(2)}, u32[]{:S(2)}) %collective-permute-start.12) | collective-permute-done | bytes 1572896 | tf_op jit(solution)/shard_map/ppermute | solution.py:12
  186.2 32.0 %collective-permute-done.13 = f32[2,48,32,128]{3,2,1,0:T(8,128)S(1)} collective-permute-done((f32[2,48,32,128]{3,2,1,0:T(8,128)S(1)}, f32[2,48,32,128]{3,2,1,0:T(8,128)S(1)}, u32[]{:S(2)}, u32[]{:S(2)}) %collective-permute-start.13) | collective-permute-done | bytes 1572896 | tf_op jit(solution)/shard_map/ppermute | solution.py:12
  220.9 33.2 %collective-permute-done.14 = f32[2,48,32,128]{3,2,1,0:T(8,128)S(1)} collective-permute-done((f32[2,48,32,128]{3,2,1,0:T(8,128)S(1)}, f32[2,48,32,128]{3,2,1,0:T(8,128)S(1)}, u32[]{:S(2)}, u32[]{:S(2)}) %collective-permute-start.14) | collective-permute-done | bytes 1572896 | tf_op jit(solution)/shard_map/ppermute | solution.py:12
  256.7 32.9 %collective-permute-done.15 = f32[2,48,32,128]{3,2,1,0:T(8,128)S(1)} collective-permute-done((f32[2,48,32,128]{3,2,1,0:T(8,128)S(1)}, f32[2,48,32,128]{3,2,1,0:T(8,128)S(1)}, u32[]{:S(2)}, u32[]{:S(2)}) %collective-permute-start.15) | collective-permute-done | bytes 1572896 | tf_op jit(solution)/shard_map/ppermute | solution.py:12
  289.6 20.8 %collective-permute-done.16 = f32[2,48,32,128]{3,2,1,0:T(8,128)} collective-permute-done((f32[2,48,32,128]{3,2,1,0:T(8,128)S(1)}, f32[2,48,32,128]{3,2,1,0:T(8,128)}, u32[]{:S(2)}, u32[]{:S(2)}) %collective-permute-start.16) | collective-permute-done | bytes 1572896 | tf_op jit(solution)/shard_map/ppermute | solution.py:12
  310.5 419.5 %while.17 = (s32[]{:T(128)}, f32[2,48,32,128]{3,2,1,0:T(8,128)}, f32[16,4]{0,1:T(4,128)}, s32[16]{0:T(128)}, s32[16]{0:T(128)}, /*index=5*/f32[2,48,32,128]{3,2,...) while((s32[]{:T(128)}, f32[2,48,32,128]{3,2,1,0:T(8,128)}, ...), condition=%wide.region_18.22_spmd.clone, body=%wide.region_0.21_spmd.clone.sunk | while | flops 9044067 | bytes 40898644 | solution.py:57
  331.0 4.2 fusion.25
  347.6 3.4 fusion.23
  355.9 5.6 fusion.25
  382.2 5.6 fusion.25
  408.3 5.6 fusion.25
  434.6 5.6 fusion.25
  460.9 5.6 fusion.25
  478.9 3.4 fusion.23
  487.1 5.6 fusion.25
  513.4 5.6 fusion.25
  539.6 5.6 fusion.25
  548.4 3.4 conditional.3
  567.0 5.6 fusion.25
  593.2 5.6 fusion.25
  619.4 5.6 fusion.25
  645.6 5.6 fusion.25
  663.6 3.4 fusion.23
  671.9 5.6 fusion.25
  698.1 5.6 fusion.25
  716.1 3.4 fusion.23
  724.3 5.6 fusion.25
  729.9 4.0 minimum_maximum_fusion
  (369 shorter events, 264.4 us)
Async XLA Ops:
  0.0 37.8 %collective-permute-start.8 = (f32[2,48,32,128]{3,2,1,0:T(8,128)}, f32[2,48,32,128]{3,2,1,0:T(8,128)S(1)}, u32[]{:S(2)}, u32[]{:S(2)}) collective-permute-start(f32[2,48,32,128]{3,2,1,0:T(8,128)} %param.33), channel_id=1, source_target_pairs={{0,31},{1,0},{2,1},{3,2},{4,3},{5,4},{6,5},{7,6},{8,7},{9,8},{10,9... | collective-permute-start | bytes 4718600 | tf_op jit(solution)/shard_map/ppermute | solution.py:12
  0.7 38.2 %collective-permute-start = (f32[2,48,32,128]{3,2,1,0:T(8,128)}, f32[2,48,32,128]{3,2,1,0:T(8,128)S(1)}, u32[]{:S(2)}, u32[]{:S(2)}) collective-permute-start(f32[2,48,32,128]{3,2,1,0:T(8,128)} %param.33), channel_id=1, source_target_pairs={{0,1},{1,2},{2,3},{3,4},{4,5},{5,6},{6,7},{7,8},{8,9},{9,10},{10,1... | collective-permute-start | bytes 4718600 | tf_op jit(solution)/shard_map/ppermute | solution.py:12
  38.9 37.0 %collective-permute-start.9 = (f32[2,48,32,128]{3,2,1,0:T(8,128)S(1)}, f32[2,48,32,128]{3,2,1,0:T(8,128)S(1)}, u32[]{:S(2)}, u32[]{:S(2)}) collective-permute-start(f32[2,48,32,128]{3,2,1,0:T(8,128)S(1)} %collective-permute-done.8), channel_id=1, source_target_pairs={{0,31},{1,0},{2,1},{3,2},{4,3},{5,4},{6,5},{7,6},{8,7},{9,8},{10,9... | collective-permute-start | bytes 4718600 | tf_op jit(solution)/shard_map/ppermute | solution.py:12
  38.9 37.0 %copy-start.1 = (f32[2,48,32,128]{3,2,1,0:T(8,128)}, f32[2,48,32,128]{3,2,1,0:T(8,128)S(1)}, u32[]{:S(2)}) copy-start(f32[2,48,32,128]{3,2,1,0:T(8,128)S(1)} %collective-permute-done) | copy-start | bytes 4718596
  38.9 37.0 %collective-permute-start.1 = (f32[2,48,32,128]{3,2,1,0:T(8,128)S(1)}, f32[2,48,32,128]{3,2,1,0:T(8,128)S(1)}, u32[]{:S(2)}, u32[]{:S(2)}) collective-permute-start(f32[2,48,32,128]{3,2,1,0:T(8,128)S(1)} %collective-permute-done), channel_id=1, source_target_pairs={{0,1},{1,2},{2,3},{3,4},{4,5},{5,6},{6,7},{7,8},{8,9},{9,10},{10,1... | collective-permute-start | bytes 4718600 | tf_op jit(solution)/shard_map/ppermute | solution.py:12
  75.9 36.7 %collective-permute-start.10 = (f32[2,48,32,128]{3,2,1,0:T(8,128)S(1)}, f32[2,48,32,128]{3,2,1,0:T(8,128)S(1)}, u32[]{:S(2)}, u32[]{:S(2)}) collective-permute-start(f32[2,48,32,128]{3,2,1,0:T(8,128)S(1)} %collective-permute-done.9), channel_id=1, source_target_pairs={{0,31},{1,0},{2,1},{3,2},{4,3},{5,4},{6,5},{7,6},{8,7},{9,8},{10,9... | collective-permute-start | bytes 4718600 | tf_op jit(solution)/shard_map/ppermute | solution.py:12
  77.1 35.6 %copy-start.3 = (f32[2,48,32,128]{3,2,1,0:T(8,128)}, f32[2,48,32,128]{3,2,1,0:T(8,128)S(1)}, u32[]{:S(2)}) copy-start(f32[2,48,32,128]{3,2,1,0:T(8,128)S(1)} %collective-permute-done.1) | copy-start | bytes 4718596
  77.1 35.6 %collective-permute-start.2 = (f32[2,48,32,128]{3,2,1,0:T(8,128)S(1)}, f32[2,48,32,128]{3,2,1,0:T(8,128)S(1)}, u32[]{:S(2)}, u32[]{:S(2)}) collective-permute-start(f32[2,48,32,128]{3,2,1,0:T(8,128)S(1)} %collective-permute-done.1), channel_id=1, source_target_pairs={{0,1},{1,2},{2,3},{3,4},{4,5},{5,6},{6,7},{7,8},{8,9},{9,10},{10,1... | collective-permute-start | bytes 4718600 | tf_op jit(solution)/shard_map/ppermute | solution.py:12
  112.7 35.8 %collective-permute-start.11 = (f32[2,48,32,128]{3,2,1,0:T(8,128)S(1)}, f32[2,48,32,128]{3,2,1,0:T(8,128)S(1)}, u32[]{:S(2)}, u32[]{:S(2)}) collective-permute-start(f32[2,48,32,128]{3,2,1,0:T(8,128)S(1)} %collective-permute-done.10), channel_id=1, source_target_pairs={{0,31},{1,0},{2,1},{3,2},{4,3},{5,4},{6,5},{7,6},{8,7},{9,8},{10,9... | collective-permute-start | bytes 4718600 | tf_op jit(solution)/shard_map/ppermute | solution.py:12
  113.9 34.7 %copy-start.5 = (f32[2,48,32,128]{3,2,1,0:T(8,128)}, f32[2,48,32,128]{3,2,1,0:T(8,128)S(1)}, u32[]{:S(2)}) copy-start(f32[2,48,32,128]{3,2,1,0:T(8,128)S(1)} %collective-permute-done.2) | copy-start | bytes 4718596
  113.9 34.7 %collective-permute-start.3 = (f32[2,48,32,128]{3,2,1,0:T(8,128)S(1)}, f32[2,48,32,128]{3,2,1,0:T(8,128)S(1)}, u32[]{:S(2)}, u32[]{:S(2)}) collective-permute-start(f32[2,48,32,128]{3,2,1,0:T(8,128)S(1)} %collective-permute-done.2), channel_id=1, source_target_pairs={{0,1},{1,2},{2,3},{3,4},{4,5},{5,6},{6,7},{7,8},{8,9},{9,10},{10,1... | collective-permute-start | bytes 4718600 | tf_op jit(solution)/shard_map/ppermute | solution.py:12
  148.5 34.9 %collective-permute-start.12 = (f32[2,48,32,128]{3,2,1,0:T(8,128)S(1)}, f32[2,48,32,128]{3,2,1,0:T(8,128)S(1)}, u32[]{:S(2)}, u32[]{:S(2)}) collective-permute-start(f32[2,48,32,128]{3,2,1,0:T(8,128)S(1)} %collective-permute-done.11), channel_id=1, source_target_pairs={{0,31},{1,0},{2,1},{3,2},{4,3},{5,4},{6,5},{7,6},{8,7},{9,8},{10,9... | collective-permute-start | bytes 4718600 | tf_op jit(solution)/shard_map/ppermute | solution.py:12
  149.7 33.8 %copy-start.7 = (f32[2,48,32,128]{3,2,1,0:T(8,128)}, f32[2,48,32,128]{3,2,1,0:T(8,128)S(1)}, u32[]{:S(2)}) copy-start(f32[2,48,32,128]{3,2,1,0:T(8,128)S(1)} %collective-permute-done.3) | copy-start | bytes 4718596
  149.7 33.8 %collective-permute-start.4 = (f32[2,48,32,128]{3,2,1,0:T(8,128)S(1)}, f32[2,48,32,128]{3,2,1,0:T(8,128)S(1)}, u32[]{:S(2)}, u32[]{:S(2)}) collective-permute-start(f32[2,48,32,128]{3,2,1,0:T(8,128)S(1)} %collective-permute-done.3), channel_id=1, source_target_pairs={{0,1},{1,2},{2,3},{3,4},{4,5},{5,6},{6,7},{7,8},{8,9},{9,10},{10,1... | collective-permute-start | bytes 4718600 | tf_op jit(solution)/shard_map/ppermute | solution.py:12
  183.5 34.7 %collective-permute-start.13 = (f32[2,48,32,128]{3,2,1,0:T(8,128)S(1)}, f32[2,48,32,128]{3,2,1,0:T(8,128)S(1)}, u32[]{:S(2)}, u32[]{:S(2)}) collective-permute-start(f32[2,48,32,128]{3,2,1,0:T(8,128)S(1)} %collective-permute-done.12), channel_id=1, source_target_pairs={{0,31},{1,0},{2,1},{3,2},{4,3},{5,4},{6,5},{7,6},{8,7},{9,8},{10,9... | collective-permute-start | bytes 4718600 | tf_op jit(solution)/shard_map/ppermute | solution.py:12
  184.6 33.5 %copy-start.9 = (f32[2,48,32,128]{3,2,1,0:T(8,128)}, f32[2,48,32,128]{3,2,1,0:T(8,128)S(1)}, u32[]{:S(2)}) copy-start(f32[2,48,32,128]{3,2,1,0:T(8,128)S(1)} %collective-permute-done.4) | copy-start | bytes 4718596
  184.6 33.5 %collective-permute-start.5 = (f32[2,48,32,128]{3,2,1,0:T(8,128)S(1)}, f32[2,48,32,128]{3,2,1,0:T(8,128)S(1)}, u32[]{:S(2)}, u32[]{:S(2)}) collective-permute-start(f32[2,48,32,128]{3,2,1,0:T(8,128)S(1)} %collective-permute-done.4), channel_id=1, source_target_pairs={{0,1},{1,2},{2,3},{3,4},{4,5},{5,6},{6,7},{7,8},{8,9},{9,10},{10,1... | collective-permute-start | bytes 4718600 | tf_op jit(solution)/shard_map/ppermute | solution.py:12
  218.2 35.9 %collective-permute-start.14 = (f32[2,48,32,128]{3,2,1,0:T(8,128)S(1)}, f32[2,48,32,128]{3,2,1,0:T(8,128)S(1)}, u32[]{:S(2)}, u32[]{:S(2)}) collective-permute-start(f32[2,48,32,128]{3,2,1,0:T(8,128)S(1)} %collective-permute-done.13), channel_id=1, source_target_pairs={{0,31},{1,0},{2,1},{3,2},{4,3},{5,4},{6,5},{7,6},{8,7},{9,8},{10,9... | collective-permute-start | bytes 4718600 | tf_op jit(solution)/shard_map/ppermute | solution.py:12
  219.3 34.7 %copy-start.11 = (f32[2,48,32,128]{3,2,1,0:T(8,128)}, f32[2,48,32,128]{3,2,1,0:T(8,128)S(1)}, u32[]{:S(2)}) copy-start(f32[2,48,32,128]{3,2,1,0:T(8,128)S(1)} %collective-permute-done.5) | copy-start | bytes 4718596
  219.3 34.8 %collective-permute-start.6 = (f32[2,48,32,128]{3,2,1,0:T(8,128)S(1)}, f32[2,48,32,128]{3,2,1,0:T(8,128)}, u32[]{:S(2)}, u32[]{:S(2)}) collective-permute-start(f32[2,48,32,128]{3,2,1,0:T(8,128)S(1)} %collective-permute-done.5), channel_id=1, source_target_pairs={{0,1},{1,2},{2,3},{3,4},{4,5},{5,6},{6,7},{7,8},{8,9},{9,10},{10,1... | collective-permute-start | bytes 4718600 | tf_op jit(solution)/shard_map/ppermute | solution.py:12
  254.1 35.5 %collective-permute-start.15 = (f32[2,48,32,128]{3,2,1,0:T(8,128)S(1)}, f32[2,48,32,128]{3,2,1,0:T(8,128)S(1)}, u32[]{:S(2)}, u32[]{:S(2)}) collective-permute-start(f32[2,48,32,128]{3,2,1,0:T(8,128)S(1)} %collective-permute-done.14), channel_id=1, source_target_pairs={{0,31},{1,0},{2,1},{3,2},{4,3},{5,4},{6,5},{7,6},{8,7},{9,8},{10,9... | collective-permute-start | bytes 4718600 | tf_op jit(solution)/shard_map/ppermute | solution.py:12
  255.2 34.4 %collective-permute-start.7 = (f32[2,48,32,128]{3,2,1,0:T(8,128)}, f32[2,48,32,128]{3,2,1,0:T(8,128)}, u32[]{:S(2)}, u32[]{:S(2)}) collective-permute-start(f32[2,48,32,128]{3,2,1,0:T(8,128)} %collective-permute-done.6), channel_id=1, source_target_pairs={{0,1},{1,2},{2,3},{3,4},{4,5},{5,6},{6,7},{7,8},{8,9},{9,10},{10,1... | collective-permute-start | bytes 4718600 | tf_op jit(solution)/shard_map/ppermute | solution.py:12
  289.6 20.8 %collective-permute-start.16 = (f32[2,48,32,128]{3,2,1,0:T(8,128)S(1)}, f32[2,48,32,128]{3,2,1,0:T(8,128)}, u32[]{:S(2)}, u32[]{:S(2)}) collective-permute-start(f32[2,48,32,128]{3,2,1,0:T(8,128)S(1)} %collective-permute-done.15), channel_id=1, source_target_pairs={{0,31},{1,0},{2,1},{3,2},{4,3},{5,4},{6,5},{7,6},{8,7},{9,8},{10,9... | collective-permute-start | bytes 4718600 | tf_op jit(solution)/shard_map/ppermute | solution.py:12
  355.9 5.6 copy-start.14
  382.2 5.6 copy-start.14
  408.3 5.6 copy-start.14
  434.6 5.6 copy-start.14
  460.9 5.6 copy-start.14
  487.1 5.6 copy-start.14
  567.0 5.6 copy-start.14
  593.2 5.6 copy-start.14
  619.4 5.6 copy-start.14
  (79 other events, 242.0 us)
where the time goes:
time: 740 us; the launch traced here: 734 us
  waiting for transfers between devices  288 us (39%)
  other arithmetic  242 us (33%)
  loops' own time  109 us (15%)
  local copies, waits for them, and re-layouts  80 us (11%)
  starting transfers between devices  14.5 us (2%)
    ppermute x17, waiting for transfers between devices, passed_along(): return lax.ppermute(x, axis, [(i, (i + by) % size) for i in range(size)])  288 us
    add x48, other arithmetic, blend(): return (1.0 - frac) * low + frac * high  115 us
    another operation x1, loops' own time, body(): best = lax.fori_loop(0, NCTRL, one_control, start)  109 us
    min x16, other arithmetic, one_control(): return jnp.minimum(best, field + control_cost[u])  88.3 us
    dynamic_slice x32, local copies, waits for them, and re-layouts, one_control(): needed = lax.switch(shard_offset[u] + REACH, branches, cell_offset[u])  39.2 us
    concatenate x16, other arithmetic, branch(): joined = jnp.concatenate([pieces[offset], pieces[offset + 1]], axis=0)  35 us
  transfers between devices with their start and end apart: 17, of which 9 were waited for; matrix products, arithmetic and copies ran while one was open for 0% of the time, Pallas kernels for 0%

commit v1 on v0

v1 whole, which is shorter than its diff:
```python
import functools

import jax
import jax.numpy as jnp
from jax import lax
from jax.experimental import pallas as pl
from jax.experimental.pallas import tpu as pltpu
from jax.sharding import PartitionSpec as P

GROUP = 8
MESH = pl.DeviceIdType.MESH
HALVES = 2
UNROLL = 4


def gather_kernel(n, value_ref, out_ref, send_sem, recv_sem, own_sem):
    me = lax.axis_index("gx")
    j = lax.rem(me, GROUP)
    base = me - j
    core = lax.rem(j, 2)

    def xor(bits):
        got = j
        for bit in (1, 2, 4):
            if bits & bit:
                got = got + bit - 2 * bit * lax.rem(got // bit, 2)
        return got

    mate, xn, yn, diag = xor(1), xor(2), xor(4), xor(6)
    first, first_to = jnp.where(core == 0, xn, yn), jnp.where(core == 0, yn, xn)
    second = first_to
    down, up = lax.rem(me + n - GROUP, n), lax.rem(me + GROUP, n)

    barrier = pltpu.get_barrier_semaphore()
    for other in (base + mate, base + xn, base + yn, down, up):
        pl.semaphore_signal(barrier, inc=1, device_id=(other,), device_id_type=MESH)
    pl.semaphore_wait(barrier, 5)

    rows, ny = value_ref.shape[0], value_ref.shape[1]
    part = ny // HALVES
    pieces = [(r, pl.ds(h * part, part)) for r in range(rows) for h in range(HALVES)]
    count = len(pieces)

    def copy(src, slot, kind, q, target):
        r, ys = pieces[q]
        return pltpu.make_async_remote_copy(
            src_ref=src.at[r, ys],
            dst_ref=out_ref.at[slot, r, ys],
            send_sem=send_sem.at[kind, q],
            recv_sem=recv_sem.at[slot, q],
            device_id=(target,),
            device_id_type=MESH,
        )

    def arrived(slot, q):
        r, ys = pieces[q]
        ref = out_ref.at[slot, r, ys]
        pltpu.make_async_copy(ref, ref, recv_sem.at[slot, q]).wait()

    def to_halo(slot, src, q):
        @pl.when(slot == 0)
        def _():
            copy(src, GROUP, 7, q, down).start()

    own = pltpu.make_async_copy(value_ref, out_ref.at[j], own_sem)
    for q in range(count):
        copy(value_ref, j, 0, q, base + first).start()
        copy(value_ref, j, 1, q, base + second).start()
        copy(value_ref, j, 2, q, base + mate).start()
        to_halo(j, value_ref, q)
    own.start()

    def take(slot, q, kinds):
        arrived(slot, q)
        src = out_ref.at[slot]
        for kind, target in kinds:
            copy(src, slot, kind, q, base + target).start()
        to_halo(slot, src, q)

    for q in range(count + 2):
        if q < count:
            take(first, q, [(3, first_to), (4, mate)])
            take(second, q, [(5, mate)])
            take(mate, q, [])
        if 1 <= q <= count:
            take(diag, q - 1, [(6, mate)])
            take(xor(3), q - 1, [])
            take(xor(5), q - 1, [])
        if q >= 2:
            take(xor(7), q - 2, [])
    for q in range(count):
        arrived(GROUP, q)
    own.wait()
    for kind in range(8):
        for q in range(count):
            copy(value_ref, j, kind, q, base + mate).wait_send()


def gather(n, value):
    rows = value.shape
    count = rows[0] * HALVES
    return pl.pallas_call(
        functools.partial(gather_kernel, n),
        out_shape=jax.ShapeDtypeStruct((GROUP + 1,) + rows, value.dtype),
        in_specs=[pl.BlockSpec(memory_space=pltpu.VMEM)],
        out_specs=pl.BlockSpec(memory_space=pl.ANY),
        scratch_shapes=[
            pltpu.SemaphoreType.DMA((8, count)),
            pltpu.SemaphoreType.DMA((GROUP + 1, count)),
            pltpu.SemaphoreType.DMA,
        ],
        compiler_params=pltpu.CompilerParams(collective_id=0, has_side_effects=True),
    )(value)


def partial_kernel(side, frac, cost, slab_at, cell_at, grid_at, src, best, held, mid, picked, sem):
    rows, ny, nz, nw = best.shape
    j = lax.rem(lax.axis_index("gx"), GROUP)
    controls = cost.shape[0]

    def place(u):
        return j + slab_at[u] + side * GROUP

    def pick(u, m):
        at = place(u)
        inside = jnp.logical_and(at >= 0, at < GROUP)

        @pl.when(inside)
        def _():
            picked[m] = u

        return m + inside.astype(jnp.int32)

    number = lax.fori_loop(0, controls, pick, 0)
    best[...] = jnp.full(best.shape, jnp.inf, jnp.float32)

    def fetch(i):
        u = picked[i]
        start = place(u) * rows + cell_at[u]
        slot = lax.rem(i, 2)
        return pltpu.make_async_copy(src.at[pl.ds(start, rows + 1)], held.at[slot], sem.at[slot])

    @pl.when(number > 0)
    def _():
        fetch(0).start()

    def one(i, carry):
        @pl.when(i + 1 < number)
        def _():
            fetch(i + 1).start()

        fetch(i).wait()
        slot = lax.rem(i, 2)
        u = picked[i]
        fx, fy, fz, fw = frac[u, 0], frac[u, 1], frac[u, 2], frac[u, 3]
        gy, gz, gw = grid_at[u, 0], grid_at[u, 1], grid_at[u, 2]
        add = cost[u]
        turn = lax.rem(nw - gw, nw)
        turn1 = lax.rem(nw - gw - 1, nw)

        def row(r, c):
            def along(y):
                y = y + gy
                y = jnp.where(y < 0, y + ny, y)
                y = jnp.where(y >= ny, y - ny, y)
                low, high = held[slot, r, y], held[slot, r + 1, y]
                return low + fx * (high - low)

            def first(b, low):
                for k in range(UNROLL):
                    y = b * UNROLL + k
                    high = along(y + 1)
                    got = low + fy * (high - low)
                    mid[y, 8:8 + nz] = got
                    mid[y, 0:8] = got[nz - 8:]
                    mid[y, 8 + nz:16 + nz] = got[:8]
                    low = high
                return low

            lax.fori_loop(0, ny // UNROLL, first, along(0))

            def second(b, c2):
                for k in range(UNROLL):
                    y = b * UNROLL + k
                    low = mid[y, pl.ds(8 + gz, nz)]
                    high = mid[y, pl.ds(9 + gz, nz)]
                    got = low + fz * (high - low)
                    low, high = pltpu.roll(got, turn, 1), pltpu.roll(got, turn1, 1)
                    got = low + fw * (high - low) + add
                    best[r, y] = jnp.minimum(best[r, y], got)
                return c2

            lax.fori_loop(0, ny // UNROLL, second, 0)
            return c

        return lax.fori_loop(0, rows, row, carry)

    lax.fori_loop(0, number, one, 0)


def partial(side, like, src, frac, cost, slab_at, cell_at, grid_at):
    rows, ny, nz, nw = like.shape
    smem = pl.BlockSpec(memory_space=pltpu.SMEM)
    flat = src.reshape((src.shape[0] * rows, ny, nz, nw))
    return pl.pallas_call(
        functools.partial(partial_kernel, side),
        out_shape=jax.ShapeDtypeStruct(like.shape, like.dtype),
        in_specs=[smem] * 5 + [pl.BlockSpec(memory_space=pl.ANY)],
        out_specs=pl.BlockSpec(memory_space=pltpu.VMEM),
        scratch_shapes=[
            pltpu.VMEM((2, rows + 1, ny, nz, nw), jnp.float32),
            pltpu.VMEM((ny, nz + 16, nw), jnp.float32),
            pltpu.SMEM((cost.shape[0],), jnp.int32),
            pltpu.SemaphoreType.DMA((2,)),
        ],
        cost_estimate=pl.CostEstimate(flops=30000000, bytes_accessed=20000000, transcendentals=0),
    )(frac, cost, slab_at, cell_at, grid_at, flat)


def passed_along(x, by):
    size = lax.axis_size("gx")
    return lax.ppermute(x, "gx", [(i, (i + by) % size) for i in range(size)])


def body(value, target, obstacle, *params):
    n = lax.axis_size("gx")
    src = gather(n, value)
    below = passed_along(partial(-1, value, src, *params), -GROUP)
    above = passed_along(partial(1, value, src, *params), GROUP)
    own = partial(0, value, src, *params)
    best = jnp.minimum(own, jnp.minimum(below, above))
    return jnp.maximum(obstacle, jnp.minimum(target, best))


def solution(mesh):
    slab = P("gx", None, None, None)
    return jax.shard_map(
        body,
        mesh=mesh,
        in_specs=(slab, slab, slab, P(), P(), P(), P(), P()),
        out_specs=slab,
        check_vma=False,
    )
```

time: 740 us -> 182 us (0.25)
  the two profiles are of different devices: /device:TPU:3 before, /device:TPU:23 now
where the time goes in v1:
time: 182 us; the launch traced here: 181 us
  Pallas kernels  145 us (80%)
  waiting for transfers between devices  27.2 us (15%)
  other arithmetic  4.45 us (2%)
  local copies, waits for them, and re-layouts  2.71 us (1%)
  starting transfers between devices  2.15 us (1%)
    pallas_call x1, Pallas kernels, gather(): pl.pallas_call(functools.partial(gather_kernel, n), out_shape=jax.ShapeDt...  79.7 us
    pallas_call x3, Pallas kernels, partial(): pl.pallas_call(functools.partial(partial_kernel, side), out_shape=jax.Sha...  64.9 us
    ppermute x2, waiting for transfers between devices, passed_along(): return lax.ppermute(x, 'gx', [(i, (i + by) % size) for i in range(size)])  27.2 us
    max x1, other arithmetic, body(): return jnp.maximum(obstacle, jnp.minimum(target, best))  4.45 us
  transfers between devices with their start and end apart: 2, of which 1 were waited for; matrix products, arithmetic and copies ran while one was open for 0% of the time, Pallas kernels for 21%

profile of v1, /device:TPU:23, one launch (start us, length us, event | category | flops | bytes accessed | tf_op | source)
XLA Modules:
  0.0 181.2 jit_solution(10928318843958568330)
XLA Ops:
  0.0 1.3 copy.9.frac
  1.3 1.4 copy.10.grid_at
  2.7 79.7 %shard_map.82 = f32[9,2,48,32,128]{4,3,2,1,0:T(8,128)} custom-call(f32[2,48,32,128]{3,2,1,0:T(8,128)} %value_ref.1), custom_call_target="tpu_custom_call" | custom-call | tf_op jit(solution)/shard_map/pallas_call | solution.py:102
  82.4 27.2 %shard_map.84 = f32[2,48,32,128]{3,2,1,0:T(8,128)} custom-call(f32[16,4]{1,0:T(8,128)} %copy.9.frac, f32[16]{0:T(128)} %cost.5, s32[16]{0:T(128)} %slab_at.5, s32[16]{0:T(128)} %cell_at.5, s32[16,3]{1,0:T(8,128)} %copy.10.grid_at, f32[18,48,32,128]{3,2,1,0:T(8,128)} %bitcast.1), custom_call_target="tpu_custom_call" | custom-call | flops 30000000 | bytes 20000000 | tf_op jit(solution)/shard_map/pallas_call | solution.py:205
  109.5 0.3 collective-permute-start
  109.8 7.3 %shard_map.85 = f32[2,48,32,128]{3,2,1,0:T(8,128)} custom-call(f32[16,4]{1,0:T(8,128)} %copy.9.frac, f32[16]{0:T(128)} %cost.5, s32[16]{0:T(128)} %slab_at.5, s32[16]{0:T(128)} %cell_at.5, s32[16,3]{1,0:T(8,128)} %copy.10.grid_at, f32[18,48,32,128]{3,2,1,0:T(8,128)} %bitcast.2), custom_call_target="tpu_custom_call" | custom-call | flops 30000000 | bytes 20000000 | tf_op jit(solution)/shard_map/pallas_call | solution.py:205
  117.1 0.0 copy-start
  117.1 0.0 copy-start.1
  117.1 1.9 %collective-permute-start.1 = (f32[2,48,32,128]{3,2,1,0:T(8,128)}, f32[2,48,32,128]{3,2,1,0:T(8,128)}, u32[]{:S(2)}, u32[]{:S(2)}) collective-permute-start(f32[2,48,32,128]{3,2,1,0:T(8,128)} %shard_map.85), channel_id=1, source_target_pairs={{0,8},{1,9},{2,10},{3,11},{4,12},{5,13},{6,14},{7,15},{8,16},{9,17... | collective-permute-start | bytes 4718600 | tf_op jit(solution)/shard_map/ppermute | solution.py:222
  119.0 30.5 %shard_map.83 = f32[2,48,32,128]{3,2,1,0:T(8,128)} custom-call(f32[16,4]{1,0:T(8,128)} %copy.9.frac, f32[16]{0:T(128)} %cost.5, s32[16]{0:T(128)} %slab_at.5, s32[16]{0:T(128)} %cell_at.5, s32[16,3]{1,0:T(8,128)} %copy.10.grid_at, f32[18,48,32,128]{3,2,1,0:T(8,128)} %bitcast.3), custom_call_target="tpu_custom_call" | custom-call | flops 30000000 | bytes 20000000 | tf_op jit(solution)/shard_map/pallas_call | solution.py:205
  149.5 0.0 collective-permute-done
  149.5 27.2 %collective-permute-done.1 = f32[2,48,32,128]{3,2,1,0:T(8,128)} collective-permute-done((f32[2,48,32,128]{3,2,1,0:T(8,128)}, f32[2,48,32,128]{3,2,1,0:T(8,128)}, u32[]{:S(2)}, u32[]{:S(2)}) %collective-permute-start.1) | collective-permute-done | bytes 1572896 | tf_op jit(solution)/shard_map/ppermute | solution.py:222
  176.7 0.0 copy-done
  176.7 0.0 copy-done.1
  176.7 4.5 %minimum_maximum_fusion = f32[2,48,32,128]{3,2,1,0:T(8,128)} fusion(f32[2,48,32,128]{3,2,1,0:T(8,128)S(1)} %copy-done, f32[2,48,32,128]{3,2,1,0:T(8,128)S(1)} %copy-done.1, f32[2,48,32,128]{3,2,1,0:T(8,128)} %shard_map.83, f32[2,48,32,128]{3,2,1,0:T(8,128)} %collective-permute-done, f32[2,48,32,128]{3,2,1,0:T(8,128)} %collective-permute-done.1), kind=kLoop, calls=%fused_computation | loop fusion | flops 1572864 | bytes 9437184 | tf_op jit(solution)/shard_map/max | solution.py:232
Async XLA Ops:
  109.5 40.0 %collective-permute-start = (f32[2,48,32,128]{3,2,1,0:T(8,128)}, f32[2,48,32,128]{3,2,1,0:T(8,128)}, u32[]{:S(2)}, u32[]{:S(2)}) collective-permute-start(f32[2,48,32,128]{3,2,1,0:T(8,128)} %shard_map.84), channel_id=1, source_target_pairs={{0,24},{1,25},{2,26},{3,27},{4,28},{5,29},{6,30},{7,31},{8,0},{9,1... | collective-permute-start | bytes 4718600 | tf_op jit(solution)/shard_map/ppermute | solution.py:222
  117.1 59.6 %copy-start = (f32[2,48,32,128]{3,2,1,0:T(8,128)S(1)}, f32[2,48,32,128]{3,2,1,0:T(8,128)}, u32[]{:S(2)}) copy-start(f32[2,48,32,128]{3,2,1,0:T(8,128)} %param.10) | copy-start | bytes 4718596
  117.1 59.6 %copy-start.1 = (f32[2,48,32,128]{3,2,1,0:T(8,128)S(1)}, f32[2,48,32,128]{3,2,1,0:T(8,128)}, u32[]{:S(2)}) copy-start(f32[2,48,32,128]{3,2,1,0:T(8,128)} %param.9) | copy-start | bytes 4718596
  117.1 59.6 %collective-permute-start.1 = (f32[2,48,32,128]{3,2,1,0:T(8,128)}, f32[2,48,32,128]{3,2,1,0:T(8,128)}, u32[]{:S(2)}, u32[]{:S(2)}) collective-permute-start(f32[2,48,32,128]{3,2,1,0:T(8,128)} %shard_map.85), channel_id=1, source_target_pairs={{0,8},{1,9},{2,10},{3,11},{4,12},{5,13},{6,14},{7,15},{8,16},{9,17... | collective-permute-start | bytes 4718600 | tf_op jit(solution)/shard_map/ppermute | solution.py:222

commit v2 on v1

--- a/solution.py
+++ b/solution.py
@@ -10,7 +10,7 @@
 GROUP = 8
 MESH = pl.DeviceIdType.MESH
 HALVES = 2
-UNROLL = 4
+UNROLL = 8
 
 
 def gather_kernel(n, value_ref, out_ref, send_sem, recv_sem, own_sem):
@@ -101,19 +101,21 @@
     count = rows[0] * HALVES
     return pl.pallas_call(
         functools.partial(gather_kernel, n),
-        out_shape=jax.ShapeDtypeStruct((GROUP + 1,) + rows, value.dtype),
+        out_shape=pltpu.VMEM((GROUP + 1,) + rows, value.dtype),
         in_specs=[pl.BlockSpec(memory_space=pltpu.VMEM)],
-        out_specs=pl.BlockSpec(memory_space=pl.ANY),
+        out_specs=pl.BlockSpec(memory_space=pltpu.VMEM),
         scratch_shapes=[
             pltpu.SemaphoreType.DMA((8, count)),
             pltpu.SemaphoreType.DMA((GROUP + 1, count)),
             pltpu.SemaphoreType.DMA,
         ],
-        compiler_params=pltpu.CompilerParams(collective_id=0, has_side_effects=True),
+        compiler_params=pltpu.CompilerParams(
+            collective_id=0, has_side_effects=True, vmem_limit_bytes=20 * 2**20
+        ),
     )(value)
 
 
-def partial_kernel(side, frac, cost, slab_at, cell_at, grid_at, src, best, held, mid, picked, sem):
+def partial_kernel(side, frac, cost, slab_at, cell_at, grid_at, src, best, mid, picked):
     rows, ny, nz, nw = best.shape
     j = lax.rem(lax.axis_index("gx"), GROUP)
     controls = cost.shape[0]
@@ -134,24 +136,9 @@
     number = lax.fori_loop(0, controls, pick, 0)
     best[...] = jnp.full(best.shape, jnp.inf, jnp.float32)
 
-    def fetch(i):
+    def one(i, carry):
         u = picked[i]
         start = place(u) * rows + cell_at[u]
-        slot = lax.rem(i, 2)
-        return pltpu.make_async_copy(src.at[pl.ds(start, rows + 1)], held.at[slot], sem.at[slot])
-
-    @pl.when(number > 0)
-    def _():
-        fetch(0).start()
-
-    def one(i, carry):
-        @pl.when(i + 1 < number)
-        def _():
-            fetch(i + 1).start()
-
-        fetch(i).wait()
-        slot = lax.rem(i, 2)
-        u = picked[i]
         fx, fy, fz, fw = frac[u, 0], frac[u, 1], frac[u, 2], frac[u, 3]
         gy, gz, gw = grid_at[u, 0], grid_at[u, 1], grid_at[u, 2]
         add = cost[u]
@@ -163,7 +150,7 @@
                 y = y + gy
                 y = jnp.where(y < 0, y + ny, y)
                 y = jnp.where(y >= ny, y - ny, y)
-                low, high = held[slot, r, y], held[slot, r + 1, y]
+                low, high = src[start + r, y], src[start + r + 1, y]
                 return low + fx * (high - low)
 
             def first(b, low):
@@ -205,14 +192,13 @@
     return pl.pallas_call(
         functools.partial(partial_kernel, side),
         out_shape=jax.ShapeDtypeStruct(like.shape, like.dtype),
-        in_specs=[smem] * 5 + [pl.BlockSpec(memory_space=pl.ANY)],
+        in_specs=[smem] * 5 + [pl.BlockSpec(memory_space=pltpu.VMEM)],
         out_specs=pl.BlockSpec(memory_space=pltpu.VMEM),
         scratch_shapes=[
-            pltpu.VMEM((2, rows + 1, ny, nz, nw), jnp.float32),
             pltpu.VMEM((ny, nz + 16, nw), jnp.float32),
             pltpu.SMEM((cost.shape[0],), jnp.int32),
-            pltpu.SemaphoreType.DMA((2,)),
         ],
+        compiler_params=pltpu.CompilerParams(vmem_limit_bytes=20 * 2**20),
         cost_estimate=pl.CostEstimate(flops=30000000, bytes_accessed=20000000, transcendentals=0),
     )(frac, cost, slab_at, cell_at, grid_at, flat)
 

time: 182 us -> 168 us (0.923); the launches traced: 181 us -> 170 us
  Pallas kernels: 145 us -> 117 us
  waiting for transfers between devices: 27.2 us -> 45.6 us
  other arithmetic: 4.45 us -> 2.11 us
    pallas_call x3, Pallas kernels: 64.9 us -> 39.2 us  [partial(): pl.pallas_call(functools.partial(partial_kernel, side), out_shape=jax.Sha...]
    ppermute x2, waiting for transfers between devices: 27.2 us -> 45.6 us  [passed_along(): return lax.ppermute(x, 'gx', [(i, (i + by) % size) for i in range(size)])]
    max x1, other arithmetic: 4.45 us -> 2.11 us  [body(): return jnp.maximum(obstacle, jnp.minimum(target, best))]
    pallas_call x1, Pallas kernels: 79.7 us -> 77.8 us  [gather(): pl.pallas_call(functools.partial(gather_kernel, n), out_shape=pltpu.VMEM(...]
  transfers between devices with their start and end apart: 2 -> 2, of which waited for: 1 -> 2; matrix products, arithmetic and copies ran while one was open for 0% -> 0% of each run, Pallas kernels for 21% -> 12%
where the time goes in v2:
time: 168 us; the launch traced here: 170 us
  Pallas kernels  117 us (70%)
  waiting for transfers between devices  45.6 us (27%)
  local copies, waits for them, and re-layouts  2.95 us (2%)
  starting transfers between devices  2.15 us (1%)
  other arithmetic  2.11 us (1%)
    pallas_call x1, Pallas kernels, gather(): pl.pallas_call(functools.partial(gather_kernel, n), out_shape=pltpu.VMEM(...  77.8 us
    ppermute x2, waiting for transfers between devices, passed_along(): return lax.ppermute(x, 'gx', [(i, (i + by) % size) for i in range(size)])  45.6 us
    pallas_call x3, Pallas kernels, partial(): pl.pallas_call(functools.partial(partial_kernel, side), out_shape=jax.Sha...  39.2 us
  transfers between devices with their start and end apart: 2, of which 2 were waited for; matrix products, arithmetic and copies ran while one was open for 0% of the time, Pallas kernels for 12%

profile of v2, /device:TPU:23, one launch (start us, length us, event | category | flops | bytes accessed | tf_op | source)
XLA Modules:
  0.0 169.9 jit_solution(9563002550201946225)
XLA Ops:
  0.0 0.8 copy.9.frac
  0.8 0.8 copy.10.grid_at
  1.5 0.0 copy-start
  1.5 1.4 copy-done
  2.9 0.0 copy-start.1
  2.9 0.0 copy-start.2
  2.9 0.0 copy-start.3
  2.9 77.8 %shard_map.82 = f32[9,2,48,32,128]{4,3,2,1,0:T(8,128)S(1)} custom-call(f32[2,48,32,128]{3,2,1,0:T(8,128)S(1)} %copy-done), custom_call_target="tpu_custom_call" | custom-call | tf_op jit(solution)/shard_map/pallas_call | solution.py:102
  80.8 0.0 copy-done.1
  80.8 0.0 copy-done.2
  80.8 0.0 copy-done.3
  80.8 19.1 %shard_map.84 = f32[2,48,32,128]{3,2,1,0:T(8,128)S(1)} custom-call(f32[16,4]{1,0:T(8,128)S(1)} %copy.9.frac, f32[16]{0:T(128)S(1)} %copy-done.1, s32[16]{0:T(128)S(1)} %copy-done.2, s32[16]{0:T(128)S(1)} %copy-done.3, s32[16,3]{1,0:T(8,128)S(1)} %copy.10.grid_at, f32[18,48,32,128]{3,2,1,0:T(8,128)S(1)} %bitcast.1), custom_call_target="tpu_custom_call" | custom-call | flops 30000000 | bytes 20000000 | tf_op jit(solution)/shard_map/pallas_call | solution.py:192
  99.9 0.3 collective-permute-start
  100.2 5.6 %shard_map.85 = f32[2,48,32,128]{3,2,1,0:T(8,128)S(1)} custom-call(f32[16,4]{1,0:T(8,128)S(1)} %copy.9.frac, f32[16]{0:T(128)S(1)} %copy-done.1, s32[16]{0:T(128)S(1)} %copy-done.2, s32[16]{0:T(128)S(1)} %copy-done.3, s32[16,3]{1,0:T(8,128)S(1)} %copy.10.grid_at, f32[18,48,32,128]{3,2,1,0:T(8,128)S(1)} %bitcast.2), custom_call_target="tpu_custom_call" | custom-call | flops 30000000 | bytes 20000000 | tf_op jit(solution)/shard_map/pallas_call | solution.py:192
  105.8 0.0 copy-start.4
  105.8 0.0 copy-start.5
  105.8 1.9 %collective-permute-start.1 = (f32[2,48,32,128]{3,2,1,0:T(8,128)S(1)}, f32[2,48,32,128]{3,2,1,0:T(8,128)S(1)}, u32[]{:S(2)}, u32[]{:S(2)}) collective-permute-start(f32[2,48,32,128]{3,2,1,0:T(8,128)S(1)} %shard_map.85), channel_id=1, source_target_pairs={{0,8},{1,9},{2,10},{3,11},{4,12},{5,13},{6,14},{7,15},{8,16},{9,17... | collective-permute-start | bytes 4718600 | tf_op jit(solution)/shard_map/ppermute | solution.py:208
  107.7 14.6 %shard_map.83 = f32[2,48,32,128]{3,2,1,0:T(8,128)S(1)} custom-call(f32[16,4]{1,0:T(8,128)S(1)} %copy.9.frac, f32[16]{0:T(128)S(1)} %copy-done.1, s32[16]{0:T(128)S(1)} %copy-done.2, s32[16]{0:T(128)S(1)} %copy-done.3, s32[16,3]{1,0:T(8,128)S(1)} %copy.10.grid_at, f32[18,48,32,128]{3,2,1,0:T(8,128)S(1)} %bitcast.3), custom_call_target="tpu_custom_call" | custom-call | flops 30000000 | bytes 20000000 | tf_op jit(solution)/shard_map/pallas_call | solution.py:192
  122.2 14.7 %collective-permute-done = f32[2,48,32,128]{3,2,1,0:T(8,128)S(1)} collective-permute-done((f32[2,48,32,128]{3,2,1,0:T(8,128)S(1)}, f32[2,48,32,128]{3,2,1,0:T(8,128)S(1)}, u32[]{:S(2)}, u32[]{:S(2)}) %collective-permute-start) | collective-permute-done | bytes 1572896 | tf_op jit(solution)/shard_map/ppermute | solution.py:208
  136.9 30.9 %collective-permute-done.1 = f32[2,48,32,128]{3,2,1,0:T(8,128)S(1)} collective-permute-done((f32[2,48,32,128]{3,2,1,0:T(8,128)S(1)}, f32[2,48,32,128]{3,2,1,0:T(8,128)S(1)}, u32[]{:S(2)}, u32[]{:S(2)}) %collective-permute-start.1) | collective-permute-done | bytes 1572896 | tf_op jit(solution)/shard_map/ppermute | solution.py:208
  167.8 0.0 copy-done.4
  167.8 0.0 copy-done.5
  167.8 2.1 %minimum_maximum_fusion = f32[2,48,32,128]{3,2,1,0:T(8,128)} fusion(f32[2,48,32,128]{3,2,1,0:T(8,128)S(1)} %copy-done.4, f32[2,48,32,128]{3,2,1,0:T(8,128)S(1)} %copy-done.5, f32[2,48,32,128]{3,2,1,0:T(8,128)S(1)} %shard_map.83, f32[2,48,32,128]{3,2,1,0:T(8,128)S(1)} %collective-permute-done, f32[2,48,32,128]{3,2,1,0:T(8,128)S(1)} %collective-permute-done.1), kind=kLoop, calls=%fused_computation | loop fusion | flops 1572864 | bytes 9437184 | tf_op jit(solution)/shard_map/max | solution.py:218
Async XLA Ops:
  1.5 1.4 copy-start
  2.9 77.8 %copy-start.1 = (f32[16]{0:T(128)S(1)}, f32[16]{0:T(128)}, u32[]{:S(2)}) copy-start(f32[16]{0:T(128)} %cost.5) | copy-start | bytes 196
  2.9 77.8 %copy-start.2 = (s32[16]{0:T(128)S(1)}, s32[16]{0:T(128)}, u32[]{:S(2)}) copy-start(s32[16]{0:T(128)} %slab_at.5) | copy-start | bytes 196
  2.9 77.9 %copy-start.3 = (s32[16]{0:T(128)S(1)}, s32[16]{0:T(128)}, u32[]{:S(2)}) copy-start(s32[16]{0:T(128)} %cell_at.5) | copy-start | bytes 196
  99.9 37.0 %collective-permute-start = (f32[2,48,32,128]{3,2,1,0:T(8,128)S(1)}, f32[2,48,32,128]{3,2,1,0:T(8,128)S(1)}, u32[]{:S(2)}, u32[]{:S(2)}) collective-permute-start(f32[2,48,32,128]{3,2,1,0:T(8,128)S(1)} %shard_map.84), channel_id=1, source_target_pairs={{0,24},{1,25},{2,26},{3,27},{4,28},{5,29},{6,30},{7,31},{8,0},{9,1... | collective-permute-start | bytes 4718600 | tf_op jit(solution)/shard_map/ppermute | solution.py:208
  105.8 62.1 %copy-start.4 = (f32[2,48,32,128]{3,2,1,0:T(8,128)S(1)}, f32[2,48,32,128]{3,2,1,0:T(8,128)}, u32[]{:S(2)}) copy-start(f32[2,48,32,128]{3,2,1,0:T(8,128)} %param.10) | copy-start | bytes 4718596
  105.8 62.0 %copy-start.5 = (f32[2,48,32,128]{3,2,1,0:T(8,128)S(1)}, f32[2,48,32,128]{3,2,1,0:T(8,128)}, u32[]{:S(2)}) copy-start(f32[2,48,32,128]{3,2,1,0:T(8,128)} %param.9) | copy-start | bytes 4718596
  105.8 62.0 %collective-permute-start.1 = (f32[2,48,32,128]{3,2,1,0:T(8,128)S(1)}, f32[2,48,32,128]{3,2,1,0:T(8,128)S(1)}, u32[]{:S(2)}, u32[]{:S(2)}) collective-permute-start(f32[2,48,32,128]{3,2,1,0:T(8,128)S(1)} %shard_map.85), channel_id=1, source_target_pairs={{0,8},{1,9},{2,10},{3,11},{4,12},{5,13},{6,14},{7,15},{8,16},{9,17... | collective-permute-start | bytes 4718600 | tf_op jit(solution)/shard_map/ppermute | solution.py:208
